TPU v7x, 32 devices: a 4x4x1 block of a 4x4x8 slice. The times are simulated.
32 devices in a mesh: dp: 1 (over z), tp2: 4 (over y), tp: 8 (over x, core).
Axes of the slice: x: 4, y: 4, z: 1, core: 2. Of those that a mesh axis runs over, the one named last changes fastest.
The devices are a block of a 4x4x8 slice.
Arguments:
- hidden: bfloat16 [512, 5120], P('dp')
- w_gate: bfloat16 [5120, 13824], P(None, ('tp', 'tp2'))
- w_up: bfloat16 [5120, 13824], P(None, ('tp', 'tp2'))
- w_down: bfloat16 [13824, 5120], P('tp', 'tp2')
- norm_gain: float32 [5120], replicated
- w_vocab: bfloat16 [5120, 32000], P('tp2', 'tp')
- temperature: float32 [512], P('dp')
- target: int32 [512], P('dp')
Outputs:
- output 1: float32 [512], P('dp')
- output 2: float32 [512], P('dp')
- output 3: float32 [512], P('dp')
- output 4: bfloat16 [512, 32000], P('dp', ('tp', 'tp2'))
All inputs are finite; a program needn't handle non-finite values.
Results may differ from a plain program's by a relative error of at most 0.00765.
Values are sent between devices in bfloat16 or wider.
A program may use at most 768 MiB of HBM per device.

v0:
```python
import jax
import jax.numpy as jnp
from jax import lax
from jax.sharding import PartitionSpec as P

NORM_EPS = 1e-6


def solution(mesh):
    tp2_size = mesh.shape['tp2']

    def device_step(hidden, w_gate, w_up, w_down, norm_gain, w_vocab, value_a11, target):
        d_model = hidden.shape[1]
        d_local = w_down.shape[1]
        tp_idx = lax.axis_index('tp')
        tp2_idx = lax.axis_index('tp2')
        gate_pre = jnp.dot(hidden, w_gate, preferred_element_type=jnp.float32)
        up_pre = jnp.dot(hidden, w_up, preferred_element_type=jnp.float32)
        act_local = (jax.nn.silu(gate_pre) * up_pre).astype(jnp.bfloat16)
        act_group = lax.all_gather(act_local, 'tp2', axis=1, tiled=True)
        y_part = jnp.dot(act_group, w_down, preferred_element_type=jnp.float32).astype(jnp.bfloat16)
        y_sum = lax.psum(y_part, 'tp')
        hid_local = lax.dynamic_slice_in_dim(hidden, tp2_idx * d_local, d_local, axis=1)
        gain_local = lax.dynamic_slice_in_dim(norm_gain, tp2_idx * d_local, d_local)
        residual = hid_local.astype(jnp.float32) + y_sum.astype(jnp.float32)
        sq_total = lax.psum(jnp.sum(residual * residual, axis=1), 'tp2')
        inv_rms = lax.rsqrt(sq_total / d_model + NORM_EPS)
        normed = (gain_local * residual * inv_rms[:, None]).astype(jnp.bfloat16)
        logit_part = jnp.dot(normed, w_vocab, preferred_element_type=jnp.float32)
        logit_sum = lax.psum_scatter(logit_part, 'tp2', scatter_dimension=1, tiled=True)
        logits = logit_sum / value_a11[:, None]
        v_local = logits.shape[1]
        col_base = (tp_idx * tp2_size + tp2_idx) * v_local
        col_ids = col_base + lax.broadcasted_iota(jnp.int32, (1, v_local), 1)
        local_max = jnp.max(logits, axis=1)
        exp_shift = jnp.exp(logits - local_max[:, None])
        local_sum = jnp.sum(exp_shift, axis=1)
        local_dot = jnp.sum(exp_shift * logits, axis=1)
        local_tgt = jnp.sum(jnp.where(col_ids == target[:, None], logits, 0.0), axis=1)
        glob_max = lax.pmax(local_max, ('tp', 'tp2'))
        rescale = jnp.exp(local_max - glob_max)
        partial_stats = jnp.stack([local_sum * rescale, local_dot * rescale, local_tgt])
        totals = lax.psum(partial_stats, ('tp', 'tp2'))
        log_norm = glob_max + jnp.log(totals[0])
        entropy = log_norm - totals[1] / totals[0]
        tgt_logp = totals[2] - log_norm
        logprobs = (logits - log_norm[:, None]).astype(jnp.bfloat16)
        return log_norm, entropy, tgt_logp, logprobs

    return jax.shard_map(device_step, mesh=mesh, in_specs=(P('dp', None), P(None, ('tp', 'tp2')), P(None, ('tp', 'tp2')), P('tp', 'tp2'), P(None), P('tp2', 'tp'), P('dp'), P('dp')), out_specs=(P('dp'), P('dp'), P('dp'), P('dp', ('tp', 'tp2'))), check_vma=False)
```

profile of v0, /device:TPU:97, one launch (start us, length us, event | category | flops | bytes accessed | tf_op | source)
XLA Modules:
  0.0 309.3 jit_solution(7008787451621498958)
XLA Ops:
  7.2 0.1 all-gather.2.cloned.1.call-start
  7.3 6.4 %fusion.11 = f32[512,432]{0,1:T(8,128)S(1)} fusion(bf16[512,5120]{1,0:T(8,128)(2,1)} %param.8, bf16[5120,432]{0,1:T(8,128)(2,1)} %param.9), kind=kOutput, calls=%fused_computation.27 | convolution fusion | flops 2264924160 | bytes 10551296 | tf_op jit(solution)/shard_map/dot_general | solution.py:17
  13.7 0.2 copy-done.6
  13.9 3.3 %fusion.4 = bf16[512,432]{0,1:T(8,128)(2,1)} fusion(bf16[512,5120]{1,0:T(8,128)(2,1)S(1)} %copy-done.2, bf16[5120,432]{0,1:T(8,128)(2,1)S(1)} %copy-done.6, f32[512,432]{0,1:T(8,128)S(1)} %fusion.11), kind=kOutput, calls=%fused_computation.13 | convolution fusion | flops 2266251264 | bytes 10993664 | tf_op jit(solution)/shard_map/dot_general | solution.py:18
  17.2 0.1 all-gather.2.cloned.1.call-update
  17.3 0.1 all-reduce.2.cloned.1.call-start
  17.3 29.1 %all-gather.2.cloned.1.call-done = bf16[512,1728]{0,1:T(8,128)(2,1)} async-done(((bf16[512,432]{0,1:T(8,128)(2,1)}), bf16[512,1728]{0,1:T(8,128)(2,1)}) %all-gather.2.cloned.1.call-update) | async-done | bytes 1769488 | tf_op jit(solution)/shard_map/all_gather | solution.py:20
  46.5 6.5 %convolution_convert_fusion = bf16[512,1280]{1,0:T(8,128)(2,1)} fusion(bf16[512,1728]{0,1:T(8,128)(2,1)} %all-gather.2.cloned.1.call-done, bf16[1728,1280]{1,0:T(8,128)(2,1)} %param.11), kind=kOutput, calls=%fused_computation | convolution fusion | flops 2265579520 | bytes 7503872 | tf_op jit(solution)/shard_map/dot_general | solution.py:21
  52.9 0.1 all-reduce.2.cloned.1.call-update
  53.0 0.1 reduce-scatter.2.cloned.1.call-start
  53.1 0.8 dynamic_slice.6
  53.8 55.5 %all-reduce.2.cloned.1.call-done = bf16[512,1280]{1,0:T(8,128)(2,1)} async-done(((bf16[512,1280]{1,0:T(8,128)(2,1)}), bf16[512,1280]{1,0:T(8,128)(2,1)}) %all-reduce.2.cloned.1.call-update) | async-done | bytes 1310736 | tf_op jit(solution)/shard_map/psum | solution.py:22
  109.4 2.3 multiply_reduce_fusion
  111.7 8.5 %psum.22 = f32[512]{0:T(512)S(1)} all-reduce(f32[512]{0:T(512)S(1)} %multiply_reduce_fusion), channel_id=1, replica_groups=mesh['dp'=1,'tp2'=4,'tp'=8] {'tp2'}, use_global_device_ids=true, to_apply=%region_2.3 | all-reduce | flops 512 | bytes 4096 | tf_op jit(solution)/shard_map/psum | solution.py:26
  120.2 10.7 %fusion.1 = f32[512,4000]{0,1:T(8,128)} fusion(bf16[1280,4000]{0,1:T(8,128)(2,1)} %param.13, bf16[512,1280]{1,0:T(8,128)(2,1)S(1)} %copy-done.1, f32[512]{0:T(512)S(1)} %add_rsqrt_fusion, f32[1280]{0:T(1024)S(1)} %dynamic_slice.6, bf16[512,5120]{1,0:T(8,128)(2,1)} %param.8, s32[]{:T(128)S(6)} %select_n.8), kind=kOutput, calls=%fused_computation.10 | convolution fusion | flops 5246812160 | bytes 21060612 | tf_op jit(solution)/shard_map/dot_general | solution.py:29
  130.9 0.1 reduce-scatter.2.cloned.1.call-update
  131.0 77.1 %reduce-scatter.2.cloned.1.call-done = f32[512,1000]{0,1:T(8,128)} async-done(((f32[512,4000]{0,1:T(8,128)}), f32[512,1000]{0,1:T(8,128)}) %reduce-scatter.2.cloned.1.call-update) | async-done | bytes 2048016 | tf_op jit(solution)/shard_map/reduce_scatter | solution.py:30
  208.1 1.9 fusion.9
  210.0 45.4 %pmax.7 = f32[512]{0:T(512)S(1)} all-reduce(f32[512]{0:T(512)S(1)} %fusion.9), channel_id=1, replica_groups=mesh['dp'=1,'tp2'=4,'tp'=8] {'tp','tp2'}, use_global_device_ids=true, to_apply=%region_5.6 | all-reduce | flops 512 | bytes 4096 | tf_op jit(solution)/shard_map/pmax | solution.py:40
  255.4 0.7 fusion
  256.1 44.2 %psum.23 = f32[3,512]{1,0:T(4,128)S(1)} all-reduce(f32[3,512]{1,0:T(4,128)S(1)} %pad_maximum_fusion), channel_id=1, replica_groups=mesh['dp'=1,'tp2'=4,'tp'=8] {'tp','tp2'}, use_global_device_ids=true, to_apply=%region_9.10 | all-reduce | flops 1536 | bytes 12288 | tf_op jit(solution)/shard_map/psum | solution.py:43
  300.4 0.6 fusion.10
  300.9 0.6 sub.28
  301.5 1.2 subtract_convert_fusion
  (18 shorter events, 0.1 us)
Async XLA Ops:
  7.2 39.3 %all-gather.2.cloned.1.call-start = ((), (), s32[]{:S(2)}) async-start(), calls=%async_computation.1 | async-start | bytes 2211840 | tf_op jit(solution)/shard_map/all_gather | solution.py:20
  7.2 6.5 %copy-start.2 = (bf16[512,5120]{1,0:T(8,128)(2,1)S(1)}, bf16[512,5120]{1,0:T(8,128)(2,1)}, u32[]{:S(2)}) copy-start(bf16[512,5120]{1,0:T(8,128)(2,1)} %param.8) | copy-start | bytes 15728644
  7.3 6.6 %copy-start.6 = (bf16[5120,432]{0,1:T(8,128)(2,1)S(1)}, bf16[5120,432]{0,1:T(8,128)(2,1)}, u32[]{:S(2)}) copy-start(bf16[5120,432]{0,1:T(8,128)(2,1)} %param.10) | copy-start | bytes 13271044
  17.3 92.1 %all-reduce.2.cloned.1.call-start = ((), (), s32[]{:S(2)}) async-start(), calls=%async_computation.2 | async-start | bytes 2621440 | tf_op jit(solution)/shard_map/psum | solution.py:22
  53.0 155.1 %reduce-scatter.2.cloned.1.call-start = ((), (), s32[]{:S(2)}) async-start(), calls=%async_computation.3 | async-start | bytes 10240000 | tf_op jit(solution)/shard_map/reduce_scatter | solution.py:30
  109.4 10.8 %copy-start.1 = (bf16[512,1280]{1,0:T(8,128)(2,1)S(1)}, bf16[512,1280]{1,0:T(8,128)(2,1)}, u32[]{:S(2)}) copy-start(bf16[512,1280]{1,0:T(8,128)(2,1)} %all-reduce.2.cloned.1.call-done) | copy-start | bytes 3932164
  130.9 77.2 %copy-start.4 = (f32[512]{0:T(512)S(1)}, f32[512]{0:T(512)}, u32[]{:S(2)}) copy-start(f32[512]{0:T(512)} %param.14) | copy-start | bytes 6148
  130.9 124.5 %copy-start.5 = (s32[512]{0:T(512)S(1)}, s32[512]{0:T(512)}, u32[]{:S(2)}) copy-start(s32[512]{0:T(512)} %param.15) | copy-start | bytes 6148
  208.1 47.3 %copy-start = (f32[512,1000]{0,1:T(8,128)S(1)}, f32[512,1000]{0,1:T(8,128)}, u32[]{:S(2)}) copy-start(f32[512,1000]{0,1:T(8,128)} %reduce-scatter.2.cloned.1.call-done) | copy-start | bytes 6144004
  300.9 1.8 copy-start.3
Sparse Core Ops, SparseCore 0:
  17.4 29.0 all-gather.1
  53.1 56.2 all-reduce.1
  131.1 76.9 reduce-scatter.1
where the time goes:
time: 310 us; the launch traced here: 309 us
  waiting for transfers between devices  162 us (52%)
  blocking collectives  98.1 us (32%)
  matrix products  26.9 us (9%)
  between operations  13.9 us (4%)
  other arithmetic  7.4 us (2%)
    reduce_scatter x1, waiting for transfers between devices, device_step(): lax.psum_scatter(logit_part, 'tp2', scatter_dimension=1, tiled=True)  77.1 us
    psum x1, waiting for transfers between devices, device_step(): y_sum = lax.psum(y_part, 'tp')  55.5 us
    pmax x1, blocking collectives, device_step(): glob_max = lax.pmax(local_max, ('tp', 'tp2'))  45.4 us
    psum x1, blocking collectives, device_step(): totals = lax.psum(partial_stats, ('tp', 'tp2'))  44.2 us
    all_gather x1, waiting for transfers between devices, device_step(): act_group = lax.all_gather(act_local, 'tp2', axis=1, tiled=True)  29.1 us
    dot_general x1, matrix products, device_step(): logit_part = jnp.dot(normed, w_vocab, preferred_element_type=jnp.float32)  10.7 us
    psum x1, blocking collectives, device_step(): sq_total = lax.psum(jnp.sum(residual * residual, axis=1), 'tp2')  8.52 us
    dot_general x1, matrix products, device_step(): jnp.dot(act_group, w_down, preferred_element_type=jnp.float32)  6.45 us
  transfers between devices with their start and end apart: 3, of which 3 were waited for; matrix products, arithmetic and copies ran while one was open for 0% of the time, Pallas kernels for 0%

commit v1 on v0

v1 whole, which is shorter than its diff:
```python
import functools

import jax
import jax.numpy as jnp
from jax import lax
from jax.experimental import pallas as pl
from jax.experimental.pallas import tpu as pltpu
from jax.sharding import PartitionSpec as P

NORM_EPS = 1e-6
ROWS = 128
LANES = 128
MESH = pl.DeviceIdType.MESH


class Sems:
    def __init__(self, ref):
        self.ref, self.used = ref, 0

    def take(self):
        self.used += 1
        return self.ref.at[self.used - 1]


def kernel(
    n2, n1,
    hidden, w_gate, w_up, w_down, gain, w_vocab, temp, target,
    out_ln, out_ent, out_tgt, out_lp,
    hid, wg, wu, wd, wv, acc_g, acc_u, act_t, yp, pair, chip, xr, ys, sq, xs,
    lg, far, mrg, dct, st2, st1,
    load_sems, send_sems, recv_sems,
):
    chunks, _, d_model = hid.shape
    ff_own = wg.shape[0]
    d_local = wd.shape[1]
    half = d_local // 2
    v_own = out_lp.shape[0]
    n_x = n1 // 2
    blk = ROWS // n_x
    y = lax.axis_index("tp2")
    tp = lax.axis_index("tp")
    x, core = tp // 2, tp % 2
    loads, sends, recvs = Sems(load_sems), Sems(send_sems), Sems(recv_sems)
    sent = []

    def at_y(j):
        return {"tp2": (y + j) % n2}

    def at_x(j):
        return {"tp": ((x + j) % n_x) * 2 + core}

    partner = {"tp": x * 2 + (1 - core)}

    def remote(src, dst, device):
        return pltpu.make_async_remote_copy(
            src_ref=src, dst_ref=dst, send_sem=sends.take(), recv_sem=recvs.take(),
            device_id=device, device_id_type=MESH,
        )

    def send(copy):
        copy.start()
        sent.append(copy)

    ff_cut = (ff_own // 2) // 16 * 16
    v_cut = (v_own // 2) // 8 * 8

    def act_rows(i, q, lo, size):
        return act_t.at[i, pl.ds(pl.multiple_of(q * ff_own + lo, 16), size), :]

    def q_of(slot):
        return (y + slot) % n2

    def base_of(slot):
        return pl.multiple_of((v_own * q_of(slot)) // 16 * 16, 16)

    def off_of(slot):
        return pl.multiple_of((v_own * q_of(slot)) % 16, 8)

    def lg_part(i, slot, part):
        lo, size = (0, v_cut) if part == 0 else (v_cut, v_own - v_cut)
        return lg.at[i, slot, pl.ds(pl.multiple_of(off_of(slot) + lo, 8), size), :]

    def part_of(buf, i, part):
        return buf.at[i, part, pl.ds(0, v_cut if part == 0 else v_own - v_cut), :]

    cps = []
    for i in range(chunks):
        c = {}
        own = act_rows(i, y, 0, ff_own)
        c["own_up"] = remote(own, own, at_y(1))
        c["own_dn"] = remote(own, own, at_y(-1))
        prev, nxt = (y + n2 - 1) % n2, (y + 1) % n2
        lo_half = act_rows(i, prev, 0, ff_cut)
        hi_half = act_rows(i, nxt, ff_cut, ff_own - ff_cut)
        c["fwd_up"] = remote(lo_half, lo_half, at_y(1))
        c["fwd_dn"] = remote(hi_half, hi_half, at_y(-1))
        c["pair"] = remote(yp.at[i, 1 - core], pair.at[i], partner)
        c["xrs"] = [
            remote(
                chip.at[i, pl.ds(pl.multiple_of(((x + j) % n_x) * blk, blk), blk), :],
                xr.at[i, j - 1], at_x(j),
            )
            for j in range(1, n_x)
        ]
        mine = ys.at[i, core, pl.ds(pl.multiple_of(x * blk, blk), blk), :]
        c["xag"] = [remote(mine, mine, at_x(j)) for j in range(1, n_x)]
        c["swap"] = remote(ys.at[i, core], ys.at[i, core], partner)
        c["ssq"] = [remote(sq.at[i, 0], sq.at[i, j], at_y(j)) for j in range(1, n2)]
        c["far_a"] = remote(lg_part(i, 2, 0), part_of(far, i, 0), at_y(-1))
        c["far_b"] = remote(lg_part(i, 2, 1), part_of(far, i, 1), at_y(1))
        c["dir_a"] = remote(lg_part(i, 1, 0), part_of(dct, i, 0), at_y(1))
        c["dir_b"] = remote(lg_part(i, 3, 1), part_of(dct, i, 1), at_y(-1))
        c["mrg_a"] = remote(lg_part(i, 3, 0), part_of(mrg, i, 0), at_y(-1))
        c["mrg_b"] = remote(lg_part(i, 1, 1), part_of(mrg, i, 1), at_y(1))
        c["st2"] = [remote(st2.at[i, 0], st2.at[i, j], at_y(j)) for j in range(1, n2)]
        c["st1"] = [
            remote(st1.at[i, 0], st1.at[i, j], {"tp": (tp + j) % n1}) for j in range(1, n1)
        ]
        cps.append(c)

    k_blocks = 4
    kb = d_model // k_blocks

    def load(src, dst):
        return pltpu.make_async_copy(src, dst, loads.take())

    ld_hid = [load(hidden.at[pl.ds(i * ROWS, ROWS), :], hid.at[i]) for i in range(chunks)]
    ld_w = [
        (
            load(w_gate.at[:, pl.ds(k * kb, kb)], wg.at[:, pl.ds(k * kb, kb)]),
            load(w_up.at[:, pl.ds(k * kb, kb)], wu.at[:, pl.ds(k * kb, kb)]),
        )
        for k in range(k_blocks)
    ]
    ld_wd = load(w_down, wd)
    ld_wv = load(w_vocab, wv)
    ld_hid[0].start()
    for pair_of in ld_w:
        for cp in pair_of:
            cp.start()
    for cp in ld_hid[1:]:
        cp.start()

    barrier = pltpu.get_barrier_semaphore()
    peers = [at_y(j) for j in range(1, n2)] + [{"tp": (tp + j) % n1} for j in range(1, n1)]
    for device in peers:
        pl.semaphore_signal(barrier, inc=1, device_id=device, device_id_type=MESH)
    pl.semaphore_wait(barrier, len(peers))

    NT = (((1,), (1,)), ((), ()))

    def gate_up(first, count):
        for i in range(first, first + count):
            ld_hid[i].wait()
        for k in range(k_blocks):
            cols = pl.ds(k * kb, kb)
            if first == 0:
                for cp in ld_w[k]:
                    cp.wait()
            h = hid[first:first + count, :, cols].reshape(count * ROWS, kb)
            g = lax.dot_general(wg[:, cols], h, NT, preferred_element_type=jnp.float32)
            u = lax.dot_general(wu[:, cols], h, NT, preferred_element_type=jnp.float32)
            if k == 0:
                acc_g[...] = g
                acc_u[...] = u
            else:
                acc_g[...] += g
                acc_u[...] += u
        act = (jax.nn.silu(acc_g[...]) * acc_u[...]).astype(jnp.bfloat16)
        for i in range(count):
            act_t[first + i, pl.ds(pl.multiple_of(y * ff_own, 16), ff_own), :] = (
                act[:, i * ROWS:(i + 1) * ROWS]
            )

    def send_own(i):
        send(cps[i]["own_up"])
        send(cps[i]["own_dn"])

    def forward(i):
        cps[i]["own_up"].wait_recv()
        send(cps[i]["fwd_up"])
        cps[i]["own_dn"].wait_recv()
        send(cps[i]["fwd_dn"])

    def down(i):
        cps[i]["fwd_up"].wait_recv()
        cps[i]["fwd_dn"].wait_recv()
        if i == 0:
            ld_wd.wait()
        for s in range(2):
            yp[i, s] = lax.dot_general(
                act_t[i], wd[:, s * half:(s + 1) * half],
                (((0,), (0,)), ((), ())), preferred_element_type=jnp.float32,
            ).astype(jnp.bfloat16)
        send(cps[i]["pair"])

    def chip_sum(i):
        cps[i]["pair"].wait_recv()
        chip[i] = (
            yp[i, core].astype(jnp.float32) + pair[i].astype(jnp.float32)
        ).astype(jnp.bfloat16)
        for cp in cps[i]["xrs"]:
            send(cp)

    def row_sum(i):
        at = pl.ds(pl.multiple_of(x * blk, blk), blk)
        total = chip[i, at, :].astype(jnp.float32)
        for j, cp in enumerate(cps[i]["xrs"]):
            cp.wait_recv()
            total += xr[i, j].astype(jnp.float32)
        ys[i, core, at, :] = total.astype(jnp.bfloat16)
        for cp in cps[i]["xag"]:
            send(cp)

    def swap(i):
        for cp in cps[i]["xag"]:
            cp.wait_recv()
        send(cps[i]["swap"])

    def residual(i, s):
        cols = pl.ds(pl.multiple_of(y * d_local + s * half, LANES), half)
        return hid[i, :, cols].astype(jnp.float32) + ys[i, s].astype(jnp.float32)

    def square(i):
        cps[i]["swap"].wait_recv()
        part = 0.0
        for s in range(2):
            r = residual(i, s)
            part = part + jnp.sum(r * r, axis=1, keepdims=True)
        sq[i, 0] = jnp.broadcast_to(part, (ROWS, LANES)).T[:8, :]
        for cp in cps[i]["ssq"]:
            send(cp)

    def norm(i):
        total = sq[i, 0]
        for j, cp in enumerate(cps[i]["ssq"]):
            cp.wait_recv()
            total = total + sq[i, j + 1]
        inv = lax.rsqrt(total / d_model + NORM_EPS)
        inv = jnp.broadcast_to(inv[:1, :], (LANES, ROWS)).T[:, :1]
        for s in range(2):
            g = gain[:, pl.ds(pl.multiple_of(y * d_local + s * half, LANES), half)]
            xs[i, :, s * half:(s + 1) * half] = (g * residual(i, s) * inv).astype(jnp.bfloat16)

    window = lg.shape[2]
    step = window // 3 if window % 48 == 0 else window

    def logits(i, slot):
        base = base_of(slot)

        @pl.loop(0, window // step)
        def _(j):
            at = pl.multiple_of(j * step, 16)
            lg[i, slot, pl.ds(at, step), :] = lax.dot_general(
                wv[pl.ds(pl.multiple_of(base + at, 16), step), :], xs[i], NT,
                preferred_element_type=jnp.float32,
            )

    def logits_far(i):
        logits(i, 2)
        send(cps[i]["far_a"])
        send(cps[i]["far_b"])

    def logits_near(i):
        logits(i, 1)
        send(cps[i]["dir_a"])
        logits(i, 3)
        send(cps[i]["dir_b"])

    def merge(i):
        for name, slot, part in (("a", 3, 0), ("b", 1, 1)):
            cps[i]["far_" + name].wait_recv()
            lg_part(i, slot, part)[...] += part_of(far, i, part)[...]
            send(cps[i]["mrg_" + name])

    def finish(i):
        logits(i, 0)
        lanes = pl.ds(i * ROWS, ROWS)
        t = temp[:, lanes]
        tgt = target[:, lanes]
        col0 = (tp * n2 + y) * v_own
        peak = None
        for part in range(2):
            cps[i]["dir_" + "ab"[part]].wait_recv()
            cps[i]["mrg_" + "ab"[part]].wait_recv()
            ref = lg_part(i, 0, part)
            val = (ref[...] + (part_of(dct, i, part)[...] + part_of(mrg, i, part)[...])) / t
            ref[...] = val
            top = jnp.max(val, axis=0, keepdims=True)
            peak = top if peak is None else jnp.maximum(peak, top)
        total = dot = hit = 0.0
        for part in range(2):
            val = lg_part(i, 0, part)[...]
            e = jnp.exp(val - peak)
            total = total + jnp.sum(e, axis=0, keepdims=True)
            dot = dot + jnp.sum(e * val, axis=0, keepdims=True)
            ids = col0 + part * v_cut + lax.broadcasted_iota(jnp.int32, val.shape, 0)
            hit = hit + jnp.sum(jnp.where(ids == tgt, val, 0.0), axis=0, keepdims=True)
        st2[i, 0, 0:1, :] = peak
        st2[i, 0, 1:2, :] = total
        st2[i, 0, 2:3, :] = dot
        st2[i, 0, 3:4, :] = hit
        st2[i, 0, 4:8, :] = jnp.zeros((4, ROWS), jnp.float32)
        for cp in cps[i]["st2"]:
            send(cp)

    def combine(tiles):
        peak = functools.reduce(jnp.maximum, [v[0:1, :] for v in tiles])
        total = dot = hit = 0.0
        for v in tiles:
            scale = jnp.exp(v[0:1, :] - peak)
            total = total + v[1:2, :] * scale
            dot = dot + v[2:3, :] * scale
            hit = hit + v[3:4, :]
        return peak, total, dot, hit

    def stats_y(i):
        for cp in cps[i]["st2"]:
            cp.wait_recv()
        vals = combine([st2[i, j] for j in range(n2)])
        for row, v in enumerate(vals):
            st1[i, 0, row:row + 1, :] = v
        st1[i, 0, 4:8, :] = jnp.zeros((4, ROWS), jnp.float32)
        for cp in cps[i]["st1"]:
            send(cp)

    def output(i):
        for cp in cps[i]["st1"]:
            cp.wait_recv()
        peak, total, dot, hit = combine([st1[i, j] for j in range(n1)])
        log_norm = peak + jnp.log(total)
        lanes = pl.ds(i * ROWS, ROWS)
        out_ln[:, lanes] = log_norm
        out_ent[:, lanes] = log_norm - dot / total
        out_tgt[:, lanes] = hit - log_norm
        val = lg[i, 0, pl.ds(off_of(0), v_own), :]
        out_lp[:, lanes] = (val - log_norm).astype(jnp.bfloat16)

    last = chunks - 1

    def run(*items):
        for fn, i in items:
            if 0 <= i <= last:
                fn(i)

    pack = acc_g.shape[1] // ROWS
    gate_up(0, pack)
    send_own(0)
    ld_wd.start()
    send_own(1)
    ld_wv.start()
    for i in range(pack, chunks, pack):
        gate_up(i, pack)
    run((forward, 0), (send_own, 2), (forward, 1), (send_own, 3))
    run((down, 0), (chip_sum, 0), (forward, 2), (down, 1), (row_sum, 0), (chip_sum, 1))
    run((forward, 3), (down, 2), (swap, 0), (row_sum, 1), (chip_sum, 2), (square, 0))
    run((down, 3), (swap, 1), (norm, 0))
    ld_wv.wait()
    run((logits_far, 0), (logits_near, 0))
    run((square, 1), (row_sum, 2), (chip_sum, 3), (norm, 1), (swap, 2), (row_sum, 3))
    run((square, 2), (swap, 3), (norm, 2), (square, 3), (norm, 3))
    for i in range(chunks):
        run((logits_far, i + 1), (merge, i), (logits_near, i + 1))
        run((finish, i - 1), (stats_y, i - 1), (output, i - 2))
    run((finish, last), (output, last - 1), (stats_y, last), (output, last))
    for cp in sent:
        cp.wait_send()


def solution(mesh):
    n2, n1 = mesh.shape["tp2"], mesh.shape["tp"]

    def device_step(hidden, w_gate, w_up, w_down, norm_gain, w_vocab, temperature, target):
        rows, d_model = hidden.shape
        ff_own = w_gate.shape[1]
        ff_tp, d_local = w_down.shape
        v_tp = w_vocab.shape[1]
        v_own = v_tp // n2
        chunks = rows // ROWS
        half = d_local // 2
        n_x = n1 // 2
        blk = ROWS // n_x
        pack = min(2, chunks)
        window = -(-v_own // 16) * 16
        part = v_own - (v_own // 2) // 8 * 8
        bf, f32 = jnp.bfloat16, jnp.float32
        n_loads = chunks + 8 + 2
        n_copies = chunks * (4 + 1 + (n_x - 1) * 2 + 1 + (n2 - 1) * 2 + 6 + n1 - 1)
        row = lambda a: a.reshape(1, -1)
        vmem = pl.BlockSpec(memory_space=pltpu.VMEM)
        hbm = pl.BlockSpec(memory_space=pl.ANY)
        ln, ent, tgt, lp = pl.pallas_call(
            functools.partial(kernel, n2, n1),
            out_shape=[
                jax.ShapeDtypeStruct((1, rows), f32),
                jax.ShapeDtypeStruct((1, rows), f32),
                jax.ShapeDtypeStruct((1, rows), f32),
                jax.ShapeDtypeStruct((v_own, rows), bf),
            ],
            in_specs=[hbm, hbm, hbm, hbm, vmem, hbm, vmem, vmem],
            out_specs=[vmem, vmem, vmem, vmem],
            scratch_shapes=[
                pltpu.VMEM((chunks, ROWS, d_model), bf),
                pltpu.VMEM((ff_own, d_model), bf),
                pltpu.VMEM((ff_own, d_model), bf),
                pltpu.VMEM((ff_tp, d_local), bf),
                pltpu.VMEM((v_tp, d_local), bf),
                pltpu.VMEM((ff_own, pack * ROWS), f32),
                pltpu.VMEM((ff_own, pack * ROWS), f32),
                pltpu.VMEM((chunks, ff_tp, ROWS), bf),
                pltpu.VMEM((chunks, 2, ROWS, half), bf),
                pltpu.VMEM((chunks, ROWS, half), bf),
                pltpu.VMEM((chunks, ROWS, half), bf),
                pltpu.VMEM((chunks, n_x - 1, blk, half), bf),
                pltpu.VMEM((chunks, 2, ROWS, half), bf),
                pltpu.VMEM((chunks, n2, 8, ROWS), f32),
                pltpu.VMEM((chunks, ROWS, d_local), bf),
                pltpu.VMEM((chunks, n2, window, ROWS), f32),
                pltpu.VMEM((chunks, 2, part, ROWS), f32),
                pltpu.VMEM((chunks, 2, part, ROWS), f32),
                pltpu.VMEM((chunks, 2, part, ROWS), f32),
                pltpu.VMEM((chunks, n2, 8, ROWS), f32),
                pltpu.VMEM((chunks, n1, 8, ROWS), f32),
                pltpu.SemaphoreType.DMA((n_loads,)),
                pltpu.SemaphoreType.DMA((n_copies,)),
                pltpu.SemaphoreType.DMA((n_copies,)),
            ],
            compiler_params=pltpu.CompilerParams(
                collective_id=0, has_side_effects=True, vmem_limit_bytes=66_000_000,
            ),
            name="decode_tail",
        )(
            hidden, w_gate.T, w_up.T, w_down, row(norm_gain), w_vocab.T,
            row(temperature), row(target),
        )
        return ln.reshape(rows), ent.reshape(rows), tgt.reshape(rows), lp.T

    return jax.shard_map(
        device_step, mesh=mesh,
        in_specs=(
            P("dp", None), P(None, ("tp", "tp2")), P(None, ("tp", "tp2")), P("tp", "tp2"),
            P(None), P("tp2", "tp"), P("dp"), P("dp"),
        ),
        out_specs=(P("dp"), P("dp"), P("dp"), P("dp", ("tp", "tp2"))),
        check_vma=False,
    )
```

time: 310 us -> 146 us (0.47)
  waiting for transfers between devices: 162 us -> 0 us
  Pallas kernels: 0 us -> 139 us
  blocking collectives: 98.1 us -> 0 us
  matrix products: 26.9 us -> 0 us
  between operations: 13.9 us -> 0.64 us
  other arithmetic: 7.4 us -> 0 us
  local copies, waits for them, and re-layouts: 0.98 us -> 5.98 us
    pallas_call x0 -> x1, Pallas kernels: none -> 139 us  [device_step(): pl.pallas_call(functools.partial(kernel, n2, n1), out_shape=[jax.ShapeDty...]
    reduce_scatter x1 -> x0, waiting for transfers between devices: 77.1 us -> none  [device_step(): lax.psum_scatter(logit_part, 'tp2', scatter_dimension=1, tiled=True)]
    psum x1 -> x0, waiting for transfers between devices: 55.5 us -> none  [device_step(): y_sum = lax.psum(y_part, 'tp')]
    psum x2 -> x0, blocking collectives: 52.7 us -> none  [the longest x1 44.2 us: device_step(): totals = lax.psum(partial_stats, ('tp', 'tp2'))]
    pmax x1 -> x0, blocking collectives: 45.4 us -> none  [device_step(): glob_max = lax.pmax(local_max, ('tp', 'tp2'))]
    all_gather x1 -> x0, waiting for transfers between devices: 29.1 us -> none  [device_step(): act_group = lax.all_gather(act_local, 'tp2', axis=1, tiled=True)]
    dot_general x4 -> x0, matrix products: 26.9 us -> none  [the longest x1 10.7 us: device_step(): logit_part = jnp.dot(normed, w_vocab, preferred_element_type=jnp.float32)]
    unnamed x14 -> x4, local copies, waits for them, and re-layouts: 0.19 us -> 5.98 us
  transfers between devices with their start and end apart: 3 -> 0, of which waited for: 3 -> 0; matrix products, arithmetic and copies ran while one was open for 0% -> 0% of each run, Pallas kernels for 0% -> 0%
where the time goes in v1:
time: 146 us; the launch traced here: 145 us
  Pallas kernels  139 us (95%)
  local copies, waits for them, and re-layouts  5.98 us (4%)
    pallas_call x1, Pallas kernels, device_step(): pl.pallas_call(functools.partial(kernel, n2, n1), out_shape=[jax.ShapeDty...  139 us
    unnamed x4, local copies, waits for them, and re-layouts  5.98 us

profile of v1, /device:TPU:97, one launch (start us, length us, event | category | flops | bytes accessed | tf_op | source)
XLA Modules:
  0.0 145.4 jit_solution(6058701890482647237)
XLA Ops:
  0.6 138.8 %decode_tail.1 = (f32[1,512]{1,0:T(1,128)}, f32[1,512]{1,0:T(1,128)}, f32[1,512]{1,0:T(1,128)}, bf16[1000,512]{1,0:T(8,128)(2,1)}) custom-call(bf16[512,5120]{1,0:T(8,128)(2,1)} %hidden.1, bf16[432,5120]{1,0:T(8,128)(2,1)} %bitcast.11, bf16[432,5120]{1,0:T(8,128)(2,1)} %bitcast.12, bf16[1728,1280]{1,0:T(8,128)(2,1)} %w_down.1, f32[1,5120]{1,0:T(1,128)} %bitcast.14, ...), custom_call_target="tpu_custom_call" | custom-call | tf_op jit(solution)/shard_map/decode_tail/pallas_call | solution.py:392
  139.5 1.3 copy.16
  140.7 1.3 copy.17
  142.0 1.2 copy.18
  143.2 2.2 %copy.19 = bf16[512,1000]{0,1:T(8,128)(2,1)} copy(bf16[512,1000]{0,1:T(8,128)(2,1)} %bitcast.13) | data formatting | bytes 2048000
